TPU v7x, 256 devices: a whole 4x4x8 slice. The times are simulated.
256 devices in a mesh: wave: 16 (over z, y_hi), lat: 16 (over x, y_lo, core).
Axes of the slice: x: 4, y: 4 (y_hi: 2, y_lo: 2; y = y_hi * 2 + y_lo), z: 8, core: 2. Of those that a mesh axis runs over, the one named last changes fastest.
Arguments:
- control: bfloat16 [640, 640, 256], P('wave', 'lat'), may hold values from -6 to 6
- vert_root: bfloat16 [640, 128, 128], P('wave'), may hold values from -0.5 to 0.5
- legendre: bfloat16 [640, 640, 256], P('lat', 'wave'), may hold values from -0.3125 to 0.3125
- row_wavenumber: int32 [640], P('wave'), may hold values from 0 to 639, each once
- courant_east: float32 [256, 1280, 128], P('wave', 'lat'), may hold values from 0.05 to 0.45
- courant_north: float32 [256, 1280, 128], P('wave', 'lat'), may hold values from 0.05 to 0.45
- east_flags: int32 [256, 1280, 128], P('wave', 'lat'), may hold values 0 or 1
- north_flags: int32 [256, 1280, 128], P('wave', 'lat'), may hold values 0 or 1
Outputs:
- tracer: float32 [256, 1280, 128], P('wave', 'lat')
Inputs may be any that keep to these rules, and one draw needn't show every extreme that they name: `row_wavenumber`: A permutation of 0 to 639.
All inputs are finite; a program needn't handle non-finite values. No bound on the sum of `east_flags` or of `north_flags` on one device may be relied on, other than what follows from the above.
Results may differ from a plain program's by a relative error of at most 0.0069.
Values may be sent and summed in bfloat16 or wider, within the bound.
No kernel may reach another device: no remote copies, remote signals or barrier semaphores. Data moves between devices by JAX's collectives and lax.ppermute only.
A program may use at most 64 MiB of HBM per device.

v0:
```python
import math
import jax
import jax.numpy as jnp
from jax import lax
from jax.sharding import PartitionSpec as P

LEV = 128
STEPS = 4


def cut_along(array, dim, length):
    shape = array.shape
    blocks = array.reshape(*shape[:dim], length, shape[dim] // length, *shape[dim + 1 :])
    return jnp.moveaxis(blocks, dim, 0)


def sum_at_owner(array, axis, dim):
    length = lax.axis_size(axis)
    blocks = lax.all_to_all(cut_along(array, dim, length), axis, 0, 0, tiled=True)
    return jnp.sum(blocks.astype(jnp.float32), axis=0)


def passed_along(value, axis, steps):
    count = lax.axis_size(axis)
    pairs = [(source, (source + steps) % count) for source in range(count)]
    return lax.ppermute(value, axis, pairs)


def passed_along_2(block, axis, distance):
    devices = range(lax.axis_size(axis))
    route = [(i - distance, i) for i in devices if i - distance in devices]
    return lax.ppermute(block, axis, route)


def with_halo(array, sides, width, wrap):
    for axis, dim in sides:
        size, length = (lax.axis_size(axis), array.shape[dim])
        up = [(i, (i + 1) % size) for i in range(size if wrap else size - 1)]
        down = [(j, i) for i, j in up]
        last = lax.slice_in_dim(array, length - width, length, axis=dim)
        leading = lax.slice_in_dim(array, 0, width, axis=dim)
        before = lax.ppermute(last, axis, up)
        after = lax.ppermute(leading, axis, down)
        array = jnp.concatenate([before, array, after], axis=dim)
    return array


def minmod(first_jump, second_jump):
    return jnp.maximum(0.0, jnp.minimum(first_jump, second_jump)) + jnp.minimum(
        0.0, jnp.maximum(first_jump, second_jump)
    )


def window(values, begin_at, end_at, axis_dim):
    return lax.slice_in_dim(values, begin_at, end_at, axis=axis_dim)


def transport(padded, winds, axis_dim, cell_count):
    jumps = window(padded, 1, cell_count + 4, axis_dim) - window(
        padded, 0, cell_count + 3, axis_dim
    )
    limited = minmod(
        window(jumps, 1, cell_count + 3, axis_dim), window(jumps, 0, cell_count + 2, axis_dim)
    )
    below_cells = window(padded, 1, cell_count + 2, axis_dim)
    above_cells = window(padded, 2, cell_count + 3, axis_dim)
    lower_slope = window(limited, 0, cell_count + 1, axis_dim)
    upper_slope = window(limited, 1, cell_count + 2, axis_dim)
    courant = jnp.abs(winds)
    fluxes = jnp.maximum(winds, 0.0) * (
        below_cells + 0.5 * (1.0 - courant) * lower_slope
    ) + jnp.minimum(winds, 0.0) * (above_cells - 0.5 * (1.0 - courant) * upper_slope)
    return window(fluxes, 1, cell_count + 1, axis_dim) - window(fluxes, 0, cell_count, axis_dim)


def dft_basis(order_ids, lon_ids, total_lon, total_orders):
    product = order_ids[:, None] * lon_ids[None, :] % total_lon
    phases = product.astype(jnp.float32) * (2.0 * math.pi / total_lon)
    weight = jnp.where(order_ids == 0, 1.0, 2.0).astype(jnp.float32) * (
        1.0 / math.sqrt(2.0 * total_orders)
    )
    return jnp.stack(
        [weight[:, None] * jnp.cos(phases), -weight[:, None] * jnp.sin(phases)]
    ).astype(jnp.bfloat16)


def per_device(
    control,
    vert_root,
    legendre,
    row_wavenumber,
    courant_east,
    courant_north,
    east_flags,
    north_flags,
):
    row_count, order_count, double_levels = control.shape
    wave_count = lax.axis_size("wave")
    lat_count = lax.axis_size("lat")
    total_orders = order_count * lat_count
    total_lon = 2 * total_orders
    level_local = LEV // wave_count
    latitudes = legendre.shape[2]
    orders = lax.axis_index("lat") * order_count + jnp.arange(order_count, dtype=jnp.int32)
    exists = row_wavenumber[:, None] >= orders[None, :]
    spectra = jnp.where(exists[:, :, None], control, jnp.zeros((), control.dtype))
    complex_parts = spectra.reshape(row_count, order_count, LEV, 2)
    vertical = jnp.einsum(
        "rmlp,rkl->kpmr", complex_parts, vert_root, preferred_element_type=jnp.float32
    ).astype(jnp.bfloat16)
    stacked = vertical.reshape(2 * LEV, order_count, row_count)
    segment = stacked
    modes_sum = sum_at_owner(
        jnp.einsum("cmr,mrj->cmj", segment, legendre, preferred_element_type=jnp.float32).astype(
            jnp.bfloat16
        ),
        "wave",
        0,
    )
    latitude_modes = modes_sum.astype(jnp.bfloat16)
    lon_local = total_lon // lat_count
    lon_ids = lax.axis_index("lat") * lon_local + jnp.arange(lon_local, dtype=jnp.int32)
    segment = lax.all_gather(latitude_modes, "lat", axis=1, tiled=True)
    order_ids = jnp.arange(segment.shape[1], dtype=jnp.int32)
    basis = dft_basis(order_ids, lon_ids, total_lon, total_orders)
    shaped = segment.reshape(level_local, 2, segment.shape[1], latitudes)
    gridded = jnp.einsum("kpmj,pml->jlk", shaped, basis, preferred_element_type=jnp.float32)
    column_tile = lax.all_to_all(gridded, "wave", split_axis=0, concat_axis=2, tiled=True)
    wind_east = courant_east * (2 * east_flags - 1).astype(jnp.float32)
    wind_north = courant_north * (2 * north_flags - 1).astype(jnp.float32)
    west_edge = passed_along(wind_east[:, -1:], "lat", 1)
    winds_x = jnp.concatenate([west_edge, wind_east], axis=1)
    south_edge = passed_along_2(wind_north[-1:], "wave", 1)
    winds_y = jnp.concatenate([south_edge, wind_north], axis=0)
    tracer = column_tile
    tile_rows = tracer.shape[0]
    tile_lon = tracer.shape[1]
    for repeat in range(STEPS):
        lon_padded = with_halo(tracer.astype(jnp.bfloat16), (("lat", 1),), 2, True).astype(
            tracer.dtype
        )
        row_padded = with_halo(tracer.astype(jnp.bfloat16), (("wave", 0),), 2, False).astype(
            tracer.dtype
        )
        tracer = (
            tracer
            - transport(lon_padded, winds_x, 1, tile_lon)
            - transport(row_padded, winds_y, 0, tile_rows)
        )
    return tracer


def solution(mesh):
    return jax.shard_map(
        per_device,
        mesh=mesh,
        in_specs=(
            P("wave", "lat", None),
            P("wave", None, None),
            P("lat", "wave", None),
            P("wave"),
            P("wave", "lat", None),
            P("wave", "lat", None),
            P("wave", "lat", None),
            P("wave", "lat", None),
        ),
        out_specs=P("wave", "lat", None),
        check_vma=False,
    )
```

profile of v0, /device:TPU:64, one launch (start us, length us, event | category | flops | bytes accessed | tf_op | source)
XLA Modules:
  0.0 311.1 jit_solution(2980356625274923959)
XLA Ops:
  7.4 1.4 broadcast_select_fusion
  8.8 4.0 %copy.54 = bf16[40,40,256]{1,0,2:T(8,128)(2,1)} copy(bf16[40,40,256]{2,1,0:T(8,128)(2,1)S(1)} %broadcast_select_fusion) | data formatting | bytes 1638400 | tf_op jit(solution)/shard_map/jit(_where)/select_n | solution.py:106
  12.8 2.7 fusion.7
  15.5 5.8 %copy.56 = bf16[128,2,40,40]{3,2,1,0:T(8,128)(2,1)} copy(bf16[128,2,40,40]{0,2,1,3:T(8,128)(2,1)S(1)} %fusion.7) | data formatting | bytes 1638400 | tf_op jit(solution)/shard_map/convert_element_type | solution.py:110
  21.3 3.3 %convolution_convert_fusion = bf16[40,256,256]{2,1,0:T(8,128)(2,1)S(1)} fusion(bf16[40,40,256]{2,1,0:T(8,128)(2,1)S(1)} %copy-done.2, bf16[256,40,40]{2,1,0:T(8,128)(2,1)} %bitcast.36), kind=kOutput, calls=%fused_computation | convolution fusion | flops 212336640 | bytes 6881280 | tf_op jit(solution)/shard_map/cmr,mrj->cmj/dot_general | solution.py:114
  25.1 128.6 %all_to_all.23 = bf16[16,16,40,256]{3,1,2,0:T(8,128)(2,1)} all-to-all(bf16[16,16,40,256]{3,1,2,0:T(8,128)(2,1)S(1)} %copy.58), channel_id=1, replica_groups=mesh['wave'=16,'lat'=16] {'wave'}, dimensions={0} | all-to-all | bytes 10485760 | tf_op jit(solution)/shard_map/all_to_all | solution.py:19
  153.7 4.0 %reduce_sum.12 = bf16[16,40,256]{2,0,1:T(8,128)(2,1)} reduce(bf16[16,16,40,256]{3,1,2,0:T(8,128)(2,1)} %all_to_all.23, bf16[]{:T(256)} %constant.23.clone.1), dimensions={0}, to_apply=%region_0.1 | reduce | flops 2457600 | bytes 5570562 | tf_op jit(solution)/shard_map/reduce_sum | solution.py:20
  158.7 37.5 %all-gather.2.cloned.1.call-done = bf16[16,640,256]{2,0,1:T(8,128)(2,1)} async-done(((bf16[16,40,256]{2,0,1:T(8,128)(2,1)}), bf16[16,640,256]{2,0,1:T(8,128)(2,1)}) %all-gather.2.cloned.1.call-update) | async-done | bytes 5242896 | tf_op jit(solution)/shard_map/all_gather | solution.py:123
  196.2 4.3 %copy.60 = bf16[16,640,256]{2,1,0:T(8,128)(2,1)S(1)} copy(bf16[16,640,256]{2,0,1:T(8,128)(2,1)} %all-gather.2.cloned.1.call-done) | data formatting | bytes 10485760 | tf_op jit(solution)/shard_map/all_gather | solution.py:123
  201.6 1.3 copy.61
  202.9 9.8 %all-to-all-start.1 = ((f32[256,80,8]{1,2,0:T(8,128)}), f32[256,80,8]{1,2,0:T(8,128)S(1)}, u32[]{:S(2)}, u32[]{:S(2)}) async-start(f32[256,80,8]{1,2,0:T(8,128)} %copy.61), calls=%async_computation.1 | async-start | bytes 2097152 | tf_op jit(solution)/shard_map/all_to_all | solution.py:128
  212.7 1.2 convert_multiply_fusion
  213.9 4.9 %collective-permute-start.3 = (f32[1,80,128]{2,1,0:T(8,128)S(1)}, f32[1,80,128]{2,1,0:T(8,128)S(1)}, u32[]{:S(2)}, u32[]{:S(2)}) collective-permute-start(f32[1,80,128]{2,1,0:T(8,128)S(1)} %slice.405), channel_id=1, source_target_pairs={{0,16},{16,32},{32,48},{48,64},{64,80},{80,96},{96,112},{112,128},... | collective-permute-start | bytes 122888 | tf_op jit(solution)/shard_map/ppermute | solution.py:32
  218.8 1.4 convert_multiply_fusion.1
  220.3 21.5 %all-to-all-done.1 = f32[256,80,8]{1,2,0:T(8,128)S(1)} async-done(((f32[256,80,8]{1,2,0:T(8,128)}), f32[256,80,8]{1,2,0:T(8,128)S(1)}, u32[]{:S(2)}, u32[]{:S(2)}) %all-to-all-start.1) | async-done | bytes 655392 | tf_op jit(solution)/shard_map/all_to_all | solution.py:128
  241.7 1.1 copy.79
  242.8 1.5 copy.66
  245.2 1.9 collective-permute-start.5
  247.2 5.4 %collective-permute-start.4 = (bf16[2,80,128]{2,1,0:T(8,128)(2,1)S(1)}, bf16[2,80,128]{2,1,0:T(8,128)(2,1)S(1)}, u32[]{:S(2)}, u32[]{:S(2)}) collective-permute-start(bf16[2,80,128]{2,1,0:T(8,128)(2,1)S(1)} %get-tuple-element.25), channel_id=1, source_target_pairs={{0,16},{16,32},{32,48},{48,64},{64,80},{80,96},{96,112},{112,128},... | collective-permute-start | bytes 122888 | tf_op jit(solution)/shard_map/ppermute | solution.py:42
  253.5 2.1 collective-permute-done.4
  256.4 2.5 collective-permute-start.7
  258.9 3.3 %collective-permute-start.9 = (bf16[2,80,128]{2,1,0:T(8,128)(2,1)S(1)}, bf16[2,80,128]{2,1,0:T(8,128)(2,1)S(1)}, u32[]{:S(2)}, u32[]{:S(2)}) collective-permute-start(bf16[2,80,128]{2,1,0:T(8,128)(2,1)S(1)} %get-tuple-element.22), channel_id=1, source_target_pairs={{16,0},{32,16},{48,32},{64,48},{80,64},{96,80},{112,96},{128,112},... | collective-permute-start | bytes 122888 | tf_op jit(solution)/shard_map/ppermute | solution.py:43
  262.2 4.1 %collective-permute-start.8 = (bf16[2,80,128]{2,1,0:T(8,128)(2,1)S(1)}, bf16[2,80,128]{2,1,0:T(8,128)(2,1)S(1)}, u32[]{:S(2)}, u32[]{:S(2)}) collective-permute-start(bf16[2,80,128]{2,1,0:T(8,128)(2,1)S(1)} %get-tuple-element.21), channel_id=1, source_target_pairs={{0,16},{16,32},{32,48},{48,64},{64,80},{80,96},{96,112},{112,128},... | collective-permute-start | bytes 122888 | tf_op jit(solution)/shard_map/ppermute | solution.py:42
  267.2 3.3 %collective-permute-done.8 = bf16[2,80,128]{2,1,0:T(8,128)(2,1)S(1)} collective-permute-done((bf16[2,80,128]{2,1,0:T(8,128)(2,1)S(1)}, bf16[2,80,128]{2,1,0:T(8,128)(2,1)S(1)}, u32[]{:S(2)}, u32[]{:S(2)}) %collective-permute-start.8) | collective-permute-done | bytes 40992 | tf_op jit(solution)/shard_map/ppermute | solution.py:42
  271.3 1.9 collective-permute-start.11
  273.2 4.9 %collective-permute-start.13 = (bf16[2,80,128]{2,1,0:T(8,128)(2,1)S(1)}, bf16[2,80,128]{2,1,0:T(8,128)(2,1)S(1)}, u32[]{:S(2)}, u32[]{:S(2)}) collective-permute-start(bf16[2,80,128]{2,1,0:T(8,128)(2,1)S(1)} %get-tuple-element.18), channel_id=1, source_target_pairs={{16,0},{32,16},{48,32},{64,48},{80,64},{96,80},{112,96},{128,112},... | collective-permute-start | bytes 122888 | tf_op jit(solution)/shard_map/ppermute | solution.py:43
  278.1 2.4 collective-permute-start.12
  281.4 5.0 %collective-permute-done.12 = bf16[2,80,128]{2,1,0:T(8,128)(2,1)S(1)} collective-permute-done((bf16[2,80,128]{2,1,0:T(8,128)(2,1)S(1)}, bf16[2,80,128]{2,1,0:T(8,128)(2,1)S(1)}, u32[]{:S(2)}, u32[]{:S(2)}) %collective-permute-start.12) | collective-permute-done | bytes 40992 | tf_op jit(solution)/shard_map/ppermute | solution.py:42
  287.2 1.9 collective-permute-start.15
  289.1 5.3 %collective-permute-start.17 = (bf16[2,80,128]{2,1,0:T(8,128)(2,1)S(1)}, bf16[2,80,128]{2,1,0:T(8,128)(2,1)S(1)}, u32[]{:S(2)}, u32[]{:S(2)}) collective-permute-start(bf16[2,80,128]{2,1,0:T(8,128)(2,1)S(1)} %get-tuple-element.14), channel_id=1, source_target_pairs={{16,0},{32,16},{48,32},{64,48},{80,64},{96,80},{112,96},{128,112},... | collective-permute-start | bytes 122888 | tf_op jit(solution)/shard_map/ppermute | solution.py:43
  294.4 2.0 collective-permute-start.16
  297.3 5.4 %collective-permute-done.16 = bf16[2,80,128]{2,1,0:T(8,128)(2,1)S(1)} collective-permute-done((bf16[2,80,128]{2,1,0:T(8,128)(2,1)S(1)}, bf16[2,80,128]{2,1,0:T(8,128)(2,1)S(1)}, u32[]{:S(2)}, u32[]{:S(2)}) %collective-permute-start.16) | collective-permute-done | bytes 40992 | tf_op jit(solution)/shard_map/ppermute | solution.py:42
  (84 shorter events, 11.5 us)
Async XLA Ops:
  6.5 6.3 %copy-start = (bf16[40,128,128]{2,1,0:T(8,128)(2,1)S(1)}, bf16[40,128,128]{2,1,0:T(8,128)(2,1)}, u32[]{:S(2)}) copy-start(bf16[40,128,128]{2,1,0:T(8,128)(2,1)} %param.9) | copy-start | bytes 3932164
  6.5 189.7 %all-gather.2.cloned.1.call-start = ((), (), s32[]{:S(2)}) async-start(), calls=%async_computation.2 | async-start | bytes 5570560 | tf_op jit(solution)/shard_map/all_gather | solution.py:123
  15.5 5.8 %copy-start.2 = (bf16[40,40,256]{2,1,0:T(8,128)(2,1)S(1)}, bf16[40,40,256]{2,1,0:T(8,128)(2,1)}, u32[]{:S(2)}) copy-start(bf16[40,40,256]{2,1,0:T(8,128)(2,1)} %param.10) | copy-start | bytes 2457604
  201.6 11.1 %copy-start.3 = (f32[16,80,128]{2,1,0:T(8,128)S(1)}, f32[16,80,128]{2,1,0:T(8,128)}, u32[]{:S(2)}) copy-start(f32[16,80,128]{2,1,0:T(8,128)} %param.13) | copy-start | bytes 1966084
  202.9 38.8 %all-to-all-start.1 = ((f32[256,80,8]{1,2,0:T(8,128)}), f32[256,80,8]{1,2,0:T(8,128)S(1)}, u32[]{:S(2)}, u32[]{:S(2)}) async-start(f32[256,80,8]{1,2,0:T(8,128)} %copy.61), calls=%async_computation.1 | async-start | bytes 2097152 | tf_op jit(solution)/shard_map/all_to_all | solution.py:128
  213.9 41.9 %collective-permute-start.3 = (f32[1,80,128]{2,1,0:T(8,128)S(1)}, f32[1,80,128]{2,1,0:T(8,128)S(1)}, u32[]{:S(2)}, u32[]{:S(2)}) collective-permute-start(f32[1,80,128]{2,1,0:T(8,128)S(1)} %slice.405), channel_id=1, source_target_pairs={{0,16},{16,32},{32,48},{48,64},{64,80},{80,96},{96,112},{112,128},... | collective-permute-start | bytes 122888 | tf_op jit(solution)/shard_map/ppermute | solution.py:32
  220.2 32.8 %collective-permute-start = (f32[16,1,128]{2,0,1:T(8,128)S(1)}, f32[16,1,128]{2,0,1:T(8,128)S(1)}, u32[]{:S(2)}, u32[]{:S(2)}) collective-permute-start(f32[16,1,128]{2,0,1:T(8,128)S(1)} %bitcast.43), channel_id=1, source_target_pairs={{0,1},{1,2},{2,3},{3,4},{4,5},{5,6},{6,7},{7,8},{8,9},{9,10},{10,1... | collective-permute-start | bytes 24584 | tf_op jit(solution)/shard_map/ppermute | solution.py:26
  244.5 2.7 collective-permute-start.2
  245.1 7.5 %collective-permute-start.1 = (bf16[16,2,128]{2,1,0:T(2,128)(2,1)S(1)}, bf16[16,2,128]{2,1,0:T(2,128)(2,1)S(1)}, u32[]{:S(2)}, u32[]{:S(2)}) collective-permute-start(bf16[16,2,128]{2,1,0:T(2,128)(2,1)S(1)} %get-tuple-element.23), channel_id=1, source_target_pairs={{0,1},{1,2},{2,3},{3,4},{4,5},{5,6},{6,7},{7,8},{8,9},{9,10},{10,1... | collective-permute-start | bytes 24584 | tf_op jit(solution)/shard_map/ppermute | solution.py:42
  245.2 8.2 %collective-permute-start.5 = (bf16[2,80,128]{2,1,0:T(8,128)(2,1)S(1)}, bf16[2,80,128]{2,1,0:T(8,128)(2,1)S(1)}, u32[]{:S(2)}, u32[]{:S(2)}) collective-permute-start(bf16[2,80,128]{2,1,0:T(8,128)(2,1)S(1)} %get-tuple-element.26), channel_id=1, source_target_pairs={{16,0},{32,16},{48,32},{64,48},{80,64},{96,80},{112,96},{128,112},... | collective-permute-start | bytes 122888 | tf_op jit(solution)/shard_map/ppermute | solution.py:43
  247.2 8.4 %collective-permute-start.4 = (bf16[2,80,128]{2,1,0:T(8,128)(2,1)S(1)}, bf16[2,80,128]{2,1,0:T(8,128)(2,1)S(1)}, u32[]{:S(2)}, u32[]{:S(2)}) collective-permute-start(bf16[2,80,128]{2,1,0:T(8,128)(2,1)S(1)} %get-tuple-element.25), channel_id=1, source_target_pairs={{0,16},{16,32},{32,48},{48,64},{64,80},{80,96},{96,112},{112,128},... | collective-permute-start | bytes 122888 | tf_op jit(solution)/shard_map/ppermute | solution.py:42
  256.4 9.9 %collective-permute-start.7 = (bf16[16,2,128]{2,1,0:T(2,128)(2,1)S(1)}, bf16[16,2,128]{2,1,0:T(2,128)(2,1)S(1)}, u32[]{:S(2)}, u32[]{:S(2)}) collective-permute-start(bf16[16,2,128]{2,1,0:T(2,128)(2,1)S(1)} %get-tuple-element.20), channel_id=1, source_target_pairs={{1,0},{2,1},{3,2},{4,3},{5,4},{6,5},{7,6},{8,7},{9,8},{10,9},{11,1... | collective-permute-start | bytes 24584 | tf_op jit(solution)/shard_map/ppermute | solution.py:43
  258.9 7.4 %collective-permute-start.6 = (bf16[16,2,128]{2,1,0:T(2,128)(2,1)S(1)}, bf16[16,2,128]{2,1,0:T(2,128)(2,1)S(1)}, u32[]{:S(2)}, u32[]{:S(2)}) collective-permute-start(bf16[16,2,128]{2,1,0:T(2,128)(2,1)S(1)} %get-tuple-element.19), channel_id=1, source_target_pairs={{0,1},{1,2},{2,3},{3,4},{4,5},{5,6},{6,7},{7,8},{8,9},{9,10},{10,1... | collective-permute-start | bytes 24584 | tf_op jit(solution)/shard_map/ppermute | solution.py:42
  258.9 8.2 %collective-permute-start.9 = (bf16[2,80,128]{2,1,0:T(8,128)(2,1)S(1)}, bf16[2,80,128]{2,1,0:T(8,128)(2,1)S(1)}, u32[]{:S(2)}, u32[]{:S(2)}) collective-permute-start(bf16[2,80,128]{2,1,0:T(8,128)(2,1)S(1)} %get-tuple-element.22), channel_id=1, source_target_pairs={{16,0},{32,16},{48,32},{64,48},{80,64},{96,80},{112,96},{128,112},... | collective-permute-start | bytes 122888 | tf_op jit(solution)/shard_map/ppermute | solution.py:43
  262.2 8.3 %collective-permute-start.8 = (bf16[2,80,128]{2,1,0:T(8,128)(2,1)S(1)}, bf16[2,80,128]{2,1,0:T(8,128)(2,1)S(1)}, u32[]{:S(2)}, u32[]{:S(2)}) collective-permute-start(bf16[2,80,128]{2,1,0:T(8,128)(2,1)S(1)} %get-tuple-element.21), channel_id=1, source_target_pairs={{0,16},{16,32},{32,48},{48,64},{64,80},{80,96},{96,112},{112,128},... | collective-permute-start | bytes 122888 | tf_op jit(solution)/shard_map/ppermute | solution.py:42
  271.3 9.3 %collective-permute-start.11 = (bf16[16,2,128]{2,1,0:T(2,128)(2,1)S(1)}, bf16[16,2,128]{2,1,0:T(2,128)(2,1)S(1)}, u32[]{:S(2)}, u32[]{:S(2)}) collective-permute-start(bf16[16,2,128]{2,1,0:T(2,128)(2,1)S(1)} %get-tuple-element.16), channel_id=1, source_target_pairs={{1,0},{2,1},{3,2},{4,3},{5,4},{6,5},{7,6},{8,7},{9,8},{10,9},{11,1... | collective-permute-start | bytes 24584 | tf_op jit(solution)/shard_map/ppermute | solution.py:43
  273.2 7.4 %collective-permute-start.10 = (bf16[16,2,128]{2,1,0:T(2,128)(2,1)S(1)}, bf16[16,2,128]{2,1,0:T(2,128)(2,1)S(1)}, u32[]{:S(2)}, u32[]{:S(2)}) collective-permute-start(bf16[16,2,128]{2,1,0:T(2,128)(2,1)S(1)} %get-tuple-element.15), channel_id=1, source_target_pairs={{0,1},{1,2},{2,3},{3,4},{4,5},{5,6},{6,7},{7,8},{8,9},{9,10},{10,1... | collective-permute-start | bytes 24584 | tf_op jit(solution)/shard_map/ppermute | solution.py:42
  273.2 8.2 %collective-permute-start.13 = (bf16[2,80,128]{2,1,0:T(8,128)(2,1)S(1)}, bf16[2,80,128]{2,1,0:T(8,128)(2,1)S(1)}, u32[]{:S(2)}, u32[]{:S(2)}) collective-permute-start(bf16[2,80,128]{2,1,0:T(8,128)(2,1)S(1)} %get-tuple-element.18), channel_id=1, source_target_pairs={{16,0},{32,16},{48,32},{64,48},{80,64},{96,80},{112,96},{128,112},... | collective-permute-start | bytes 122888 | tf_op jit(solution)/shard_map/ppermute | solution.py:43
  278.1 8.3 %collective-permute-start.12 = (bf16[2,80,128]{2,1,0:T(8,128)(2,1)S(1)}, bf16[2,80,128]{2,1,0:T(8,128)(2,1)S(1)}, u32[]{:S(2)}, u32[]{:S(2)}) collective-permute-start(bf16[2,80,128]{2,1,0:T(8,128)(2,1)S(1)} %get-tuple-element.17), channel_id=1, source_target_pairs={{0,16},{16,32},{32,48},{48,64},{64,80},{80,96},{96,112},{112,128},... | collective-permute-start | bytes 122888 | tf_op jit(solution)/shard_map/ppermute | solution.py:42
  287.2 9.3 %collective-permute-start.15 = (bf16[16,2,128]{2,1,0:T(2,128)(2,1)S(1)}, bf16[16,2,128]{2,1,0:T(2,128)(2,1)S(1)}, u32[]{:S(2)}, u32[]{:S(2)}) collective-permute-start(bf16[16,2,128]{2,1,0:T(2,128)(2,1)S(1)} %get-tuple-element.12), channel_id=1, source_target_pairs={{1,0},{2,1},{3,2},{4,3},{5,4},{6,5},{7,6},{8,7},{9,8},{10,9},{11,1... | collective-permute-start | bytes 24584 | tf_op jit(solution)/shard_map/ppermute | solution.py:43
  289.1 7.4 %collective-permute-start.14 = (bf16[16,2,128]{2,1,0:T(2,128)(2,1)S(1)}, bf16[16,2,128]{2,1,0:T(2,128)(2,1)S(1)}, u32[]{:S(2)}, u32[]{:S(2)}) collective-permute-start(bf16[16,2,128]{2,1,0:T(2,128)(2,1)S(1)} %get-tuple-element.11), channel_id=1, source_target_pairs={{0,1},{1,2},{2,3},{3,4},{4,5},{5,6},{6,7},{7,8},{8,9},{9,10},{10,1... | collective-permute-start | bytes 24584 | tf_op jit(solution)/shard_map/ppermute | solution.py:42
  289.1 8.2 %collective-permute-start.17 = (bf16[2,80,128]{2,1,0:T(8,128)(2,1)S(1)}, bf16[2,80,128]{2,1,0:T(8,128)(2,1)S(1)}, u32[]{:S(2)}, u32[]{:S(2)}) collective-permute-start(bf16[2,80,128]{2,1,0:T(8,128)(2,1)S(1)} %get-tuple-element.14), channel_id=1, source_target_pairs={{16,0},{32,16},{48,32},{64,48},{80,64},{96,80},{112,96},{128,112},... | collective-permute-start | bytes 122888 | tf_op jit(solution)/shard_map/ppermute | solution.py:43
  294.4 8.3 %collective-permute-start.16 = (bf16[2,80,128]{2,1,0:T(8,128)(2,1)S(1)}, bf16[2,80,128]{2,1,0:T(8,128)(2,1)S(1)}, u32[]{:S(2)}, u32[]{:S(2)}) collective-permute-start(bf16[2,80,128]{2,1,0:T(8,128)(2,1)S(1)} %get-tuple-element.13), channel_id=1, source_target_pairs={{0,16},{16,32},{32,48},{48,64},{64,80},{80,96},{96,112},{112,128},... | collective-permute-start | bytes 122888 | tf_op jit(solution)/shard_map/ppermute | solution.py:42
  303.0 1.3 copy-start.1
Sparse Core Ops, SparseCore 0:
  157.9 38.2 all-gather.1
where the time goes:
time: 312 us; the launch traced here: 311 us
  blocking collectives  129 us (41%)
  waiting for transfers between devices  74.9 us (24%)
  starting transfers between devices  51.2 us (16%)
  local copies, waits for them, and re-layouts  18.7 us (6%)
  other arithmetic  16.8 us (5%)
  between operations  14 us (4%)
  matrix products  6.99 us (2%)
    all_to_all x1, blocking collectives, sum_at_owner(): lax.all_to_all(cut_along(array, dim, length), axis, 0, 0, tiled=True)  129 us
    all_gather x1, waiting for transfers between devices, per_device(): segment = lax.all_gather(latitude_modes, 'lat', axis=1, tiled=True)  37.5 us
    ppermute x8, starting transfers between devices, with_halo(): after = lax.ppermute(leading, axis, down)  22.4 us
    all_to_all x1, waiting for transfers between devices, per_device(): lax.all_to_all(gridded, 'wave', split_axis=0, concat_axis=2, tiled=True)  21.5 us
    ppermute x8, waiting for transfers between devices, with_halo(): before = lax.ppermute(last, axis, up)  15.9 us
    ppermute x8, starting transfers between devices, with_halo(): before = lax.ppermute(last, axis, up)  14.1 us
    all_to_all x1, starting transfers between devices, per_device(): lax.all_to_all(gridded, 'wave', split_axis=0, concat_axis=2, tiled=True)  9.8 us
  transfers between devices with their start and end apart: 20, of which 6 were waited for; matrix products, arithmetic and copies ran while one was open for 3% of the time, Pallas kernels for 0%

commit v1 on v0

--- a/solution.py
+++ b/solution.py
@@ -120,7 +120,10 @@
     latitude_modes = modes_sum.astype(jnp.bfloat16)
     lon_local = total_lon // lat_count
     lon_ids = lax.axis_index("lat") * lon_local + jnp.arange(lon_local, dtype=jnp.int32)
-    segment = lax.all_gather(latitude_modes, "lat", axis=1, tiled=True)
+    n_dev = lax.axis_size("lat")
+    pieces = jnp.stack([latitude_modes for _ in range(n_dev)])
+    pieces = lax.all_to_all(pieces, "lat", split_axis=0, concat_axis=0)
+    segment = jnp.concatenate(pieces, axis=1)
     order_ids = jnp.arange(segment.shape[1], dtype=jnp.int32)
     basis = dft_basis(order_ids, lon_ids, total_lon, total_orders)
     shaped = segment.reshape(level_local, 2, segment.shape[1], latitudes)

time: 312 us -> 339 us (1.087)
  waiting for transfers between devices: 74.9 us -> 113 us
  between operations: 14 us -> 0.6 us
    all_to_all x0 -> x1, waiting for transfers between devices: none -> 75.2 us  [per_device(): pieces = lax.all_to_all(pieces, 'lat', split_axis=0, concat_axis=0)]
    all_gather x1 -> x0, waiting for transfers between devices: 37.5 us -> none  [per_device(): segment = lax.all_gather(latitude_modes, 'lat', axis=1, tiled=True)]
    all_to_all x0 -> x1, starting transfers between devices: none -> 4.59 us  [per_device(): pieces = lax.all_to_all(pieces, 'lat', split_axis=0, concat_axis=0)]
    all_gather x1 -> x0, local copies, waits for them, and re-layouts: 4.34 us -> none  [per_device(): segment = lax.all_gather(latitude_modes, 'lat', axis=1, tiled=True)]
    all_to_all x1, starting transfers between devices: 9.8 us -> 5.58 us  [per_device(): lax.all_to_all(gridded, 'wave', split_axis=0, concat_axis=2, tiled=True)]
where the time goes in v1:
time: 339 us; the launch traced here: 337 us
  blocking collectives  129 us (38%)
  waiting for transfers between devices  113 us (33%)
  starting transfers between devices  51.6 us (15%)
  local copies, waits for them, and re-layouts  20.4 us (6%)
  other arithmetic  16.1 us (5%)
  matrix products  6.98 us (2%)
    all_to_all x1, blocking collectives, sum_at_owner(): lax.all_to_all(cut_along(array, dim, length), axis, 0, 0, tiled=True)  129 us
    all_to_all x1, waiting for transfers between devices, per_device(): pieces = lax.all_to_all(pieces, 'lat', split_axis=0, concat_axis=0)  75.2 us
    ppermute x8, starting transfers between devices, with_halo(): after = lax.ppermute(leading, axis, down)  22.3 us
    all_to_all x1, waiting for transfers between devices, per_device(): lax.all_to_all(gridded, 'wave', split_axis=0, concat_axis=2, tiled=True)  21.3 us
    ppermute x8, waiting for transfers between devices, with_halo(): before = lax.ppermute(last, axis, up)  16.1 us
    ppermute x8, starting transfers between devices, with_halo(): before = lax.ppermute(last, axis, up)  14.2 us
  transfers between devices with their start and end apart: 20, of which 6 were waited for; matrix products, arithmetic and copies ran while one was open for 3% of the time, Pallas kernels for 0%

profile of v1, /device:TPU:64, one launch (start us, length us, event | category | flops | bytes accessed | tf_op | source)
XLA Modules:
  0.0 336.9 jit_solution(12753860186790740476)
XLA Ops:
  0.8 1.4 broadcast_select_fusion
  2.3 4.0 %copy.39 = bf16[40,40,256]{1,0,2:T(8,128)(2,1)} copy(bf16[40,40,256]{2,1,0:T(8,128)(2,1)S(1)} %broadcast_select_fusion) | data formatting | bytes 1638400 | tf_op jit(solution)/shard_map/jit(_where)/select_n | solution.py:106
  6.3 2.7 fusion.7
  9.0 5.8 %copy.41 = bf16[128,2,40,40]{3,2,1,0:T(8,128)(2,1)} copy(bf16[128,2,40,40]{0,2,1,3:T(8,128)(2,1)S(1)} %fusion.7) | data formatting | bytes 1638400 | tf_op jit(solution)/shard_map/convert_element_type | solution.py:110
  14.8 3.2 convolution_convert_fusion
  18.6 128.6 %all_to_all.28 = bf16[16,16,40,256]{3,1,2,0:T(8,128)(2,1)} all-to-all(bf16[16,16,40,256]{3,1,2,0:T(8,128)(2,1)S(1)} %copy.43), channel_id=1, replica_groups=mesh['wave'=16,'lat'=16] {'wave'}, dimensions={0} | all-to-all | bytes 10485760 | tf_op jit(solution)/shard_map/all_to_all | solution.py:19
  147.1 3.3 reduce_sum.12
  150.6 2.9 stack.6
  153.5 4.6 %all-to-all-start.1 = ((bf16[16,16,40,256]{3,2,1,0:T(8,128)(2,1)}), bf16[16,16,40,256]{3,2,1,0:T(8,128)(2,1)}, u32[]{:S(2)}, u32[]{:S(2)}) async-start(bf16[16,16,40,256]{3,2,1,0:T(8,128)(2,1)} %stack.6), calls=%async_computation.1 | async-start | bytes 10485760 | tf_op jit(solution)/shard_map/all_to_all | solution.py:125
  159.1 75.2 %all-to-all-done.1 = bf16[16,16,40,256]{3,2,1,0:T(8,128)(2,1)} async-done(((bf16[16,16,40,256]{3,2,1,0:T(8,128)(2,1)}), bf16[16,16,40,256]{3,2,1,0:T(8,128)(2,1)}, u32[]{:S(2)}, u32[]{:S(2)}) %all-to-all-start.1) | async-done | bytes 5242912 | tf_op jit(solution)/shard_map/all_to_all | solution.py:125
  234.2 3.0 copy.46
  238.3 1.3 copy.47
  239.6 5.6 %all-to-all-start.2 = ((f32[256,80,8]{1,2,0:T(8,128)}), f32[256,80,8]{1,2,0:T(8,128)S(1)}, u32[]{:S(2)}, u32[]{:S(2)}) async-start(f32[256,80,8]{1,2,0:T(8,128)} %copy.47), calls=%async_computation.2 | async-start | bytes 2097152 | tf_op jit(solution)/shard_map/all_to_all | solution.py:131
  246.4 4.9 %collective-permute-start.3 = (f32[1,80,128]{2,1,0:T(8,128)S(1)}, f32[1,80,128]{2,1,0:T(8,128)S(1)}, u32[]{:S(2)}, u32[]{:S(2)}) collective-permute-start(f32[1,80,128]{2,1,0:T(8,128)S(1)} %slice.405), channel_id=1, source_target_pairs={{0,16},{16,32},{32,48},{48,64},{64,80},{80,96},{96,112},{112,128},... | collective-permute-start | bytes 122888 | tf_op jit(solution)/shard_map/ppermute | solution.py:32
  251.3 1.4 convert_multiply_fusion.1
  252.8 21.3 %all-to-all-done.2 = f32[256,80,8]{1,2,0:T(8,128)S(1)} async-done(((f32[256,80,8]{1,2,0:T(8,128)}), f32[256,80,8]{1,2,0:T(8,128)S(1)}, u32[]{:S(2)}, u32[]{:S(2)}) %all-to-all-start.2) | async-done | bytes 655392 | tf_op jit(solution)/shard_map/all_to_all | solution.py:131
  275.2 1.5 copy.52
  277.4 1.9 collective-permute-start.5
  279.3 5.4 %collective-permute-start.4 = (bf16[2,80,128]{2,1,0:T(8,128)(2,1)S(1)}, bf16[2,80,128]{2,1,0:T(8,128)(2,1)S(1)}, u32[]{:S(2)}, u32[]{:S(2)}) collective-permute-start(bf16[2,80,128]{2,1,0:T(8,128)(2,1)S(1)} %get-tuple-element.25), channel_id=1, source_target_pairs={{0,16},{16,32},{32,48},{48,64},{64,80},{80,96},{96,112},{112,128},... | collective-permute-start | bytes 122888 | tf_op jit(solution)/shard_map/ppermute | solution.py:42
  285.6 2.1 collective-permute-done.4
  288.5 2.6 collective-permute-start.7
  291.1 3.6 %collective-permute-start.9 = (bf16[2,80,128]{2,1,0:T(8,128)(2,1)S(1)}, bf16[2,80,128]{2,1,0:T(8,128)(2,1)S(1)}, u32[]{:S(2)}, u32[]{:S(2)}) collective-permute-start(bf16[2,80,128]{2,1,0:T(8,128)(2,1)S(1)} %get-tuple-element.22), channel_id=1, source_target_pairs={{16,0},{32,16},{48,32},{64,48},{80,64},{96,80},{112,96},{128,112},... | collective-permute-start | bytes 122888 | tf_op jit(solution)/shard_map/ppermute | solution.py:43
  294.7 3.8 %collective-permute-start.8 = (bf16[2,80,128]{2,1,0:T(8,128)(2,1)S(1)}, bf16[2,80,128]{2,1,0:T(8,128)(2,1)S(1)}, u32[]{:S(2)}, u32[]{:S(2)}) collective-permute-start(bf16[2,80,128]{2,1,0:T(8,128)(2,1)S(1)} %get-tuple-element.21), channel_id=1, source_target_pairs={{0,16},{16,32},{32,48},{48,64},{64,80},{80,96},{96,112},{112,128},... | collective-permute-start | bytes 122888 | tf_op jit(solution)/shard_map/ppermute | solution.py:42
  299.3 3.7 %collective-permute-done.8 = bf16[2,80,128]{2,1,0:T(8,128)(2,1)S(1)} collective-permute-done((bf16[2,80,128]{2,1,0:T(8,128)(2,1)S(1)}, bf16[2,80,128]{2,1,0:T(8,128)(2,1)S(1)}, u32[]{:S(2)}, u32[]{:S(2)}) %collective-permute-start.8) | collective-permute-done | bytes 40992 | tf_op jit(solution)/shard_map/ppermute | solution.py:42
  303.7 1.9 collective-permute-start.11
  305.6 5.6 %collective-permute-start.13 = (bf16[2,80,128]{2,1,0:T(8,128)(2,1)S(1)}, bf16[2,80,128]{2,1,0:T(8,128)(2,1)S(1)}, u32[]{:S(2)}, u32[]{:S(2)}) collective-permute-start(bf16[2,80,128]{2,1,0:T(8,128)(2,1)S(1)} %get-tuple-element.18), channel_id=1, source_target_pairs={{16,0},{32,16},{48,32},{64,48},{80,64},{96,80},{112,96},{128,112},... | collective-permute-start | bytes 122888 | tf_op jit(solution)/shard_map/ppermute | solution.py:43
  311.3 1.9 collective-permute-start.12
  314.1 5.5 %collective-permute-done.12 = bf16[2,80,128]{2,1,0:T(8,128)(2,1)S(1)} collective-permute-done((bf16[2,80,128]{2,1,0:T(8,128)(2,1)S(1)}, bf16[2,80,128]{2,1,0:T(8,128)(2,1)S(1)}, u32[]{:S(2)}, u32[]{:S(2)}) %collective-permute-start.12) | collective-permute-done | bytes 40992 | tf_op jit(solution)/shard_map/ppermute | solution.py:42
  320.3 1.9 collective-permute-start.15
  322.2 4.8 %collective-permute-start.17 = (bf16[2,80,128]{2,1,0:T(8,128)(2,1)S(1)}, bf16[2,80,128]{2,1,0:T(8,128)(2,1)S(1)}, u32[]{:S(2)}, u32[]{:S(2)}) collective-permute-start(bf16[2,80,128]{2,1,0:T(8,128)(2,1)S(1)} %get-tuple-element.14), channel_id=1, source_target_pairs={{16,0},{32,16},{48,32},{64,48},{80,64},{96,80},{112,96},{128,112},... | collective-permute-start | bytes 122888 | tf_op jit(solution)/shard_map/ppermute | solution.py:43
  327.0 2.6 collective-permute-start.16
  330.5 4.8 %collective-permute-done.16 = bf16[2,80,128]{2,1,0:T(8,128)(2,1)S(1)} collective-permute-done((bf16[2,80,128]{2,1,0:T(8,128)(2,1)S(1)}, bf16[2,80,128]{2,1,0:T(8,128)(2,1)S(1)}, u32[]{:S(2)}, u32[]{:S(2)}) %collective-permute-start.16) | collective-permute-done | bytes 40992 | tf_op jit(solution)/shard_map/ppermute | solution.py:42
  (85 shorter events, 13.6 us)
Async XLA Ops:
  0.0 6.3 %copy-start = (bf16[40,128,128]{2,1,0:T(8,128)(2,1)S(1)}, bf16[40,128,128]{2,1,0:T(8,128)(2,1)}, u32[]{:S(2)}) copy-start(bf16[40,128,128]{2,1,0:T(8,128)(2,1)} %param.9) | copy-start | bytes 3932164
  9.0 5.8 %copy-start.2 = (bf16[40,40,256]{2,1,0:T(8,128)(2,1)S(1)}, bf16[40,40,256]{2,1,0:T(8,128)(2,1)}, u32[]{:S(2)}) copy-start(bf16[40,40,256]{2,1,0:T(8,128)(2,1)} %param.10) | copy-start | bytes 2457604
  153.5 80.7 %all-to-all-start.1 = ((bf16[16,16,40,256]{3,2,1,0:T(8,128)(2,1)}), bf16[16,16,40,256]{3,2,1,0:T(8,128)(2,1)}, u32[]{:S(2)}, u32[]{:S(2)}) async-start(bf16[16,16,40,256]{3,2,1,0:T(8,128)(2,1)} %stack.6), calls=%async_computation.1 | async-start | bytes 10485760 | tf_op jit(solution)/shard_map/all_to_all | solution.py:125
  238.3 6.9 %copy-start.3 = (f32[16,80,128]{2,1,0:T(8,128)S(1)}, f32[16,80,128]{2,1,0:T(8,128)}, u32[]{:S(2)}) copy-start(f32[16,80,128]{2,1,0:T(8,128)} %param.13) | copy-start | bytes 1966084
  239.6 34.5 %all-to-all-start.2 = ((f32[256,80,8]{1,2,0:T(8,128)}), f32[256,80,8]{1,2,0:T(8,128)S(1)}, u32[]{:S(2)}, u32[]{:S(2)}) async-start(f32[256,80,8]{1,2,0:T(8,128)} %copy.47), calls=%async_computation.2 | async-start | bytes 2097152 | tf_op jit(solution)/shard_map/all_to_all | solution.py:131
  246.4 41.6 %collective-permute-start.3 = (f32[1,80,128]{2,1,0:T(8,128)S(1)}, f32[1,80,128]{2,1,0:T(8,128)S(1)}, u32[]{:S(2)}, u32[]{:S(2)}) collective-permute-start(f32[1,80,128]{2,1,0:T(8,128)S(1)} %slice.405), channel_id=1, source_target_pairs={{0,16},{16,32},{32,48},{48,64},{64,80},{80,96},{96,112},{112,128},... | collective-permute-start | bytes 122888 | tf_op jit(solution)/shard_map/ppermute | solution.py:32
  252.7 32.5 %collective-permute-start = (f32[16,1,128]{2,0,1:T(8,128)S(1)}, f32[16,1,128]{2,0,1:T(8,128)S(1)}, u32[]{:S(2)}, u32[]{:S(2)}) collective-permute-start(f32[16,1,128]{2,0,1:T(8,128)S(1)} %bitcast.44), channel_id=1, source_target_pairs={{0,1},{1,2},{2,3},{3,4},{4,5},{5,6},{6,7},{7,8},{8,9},{9,10},{10,1... | collective-permute-start | bytes 24584 | tf_op jit(solution)/shard_map/ppermute | solution.py:26
  276.8 2.5 collective-permute-start.2
  276.9 7.9 %collective-permute-start.1 = (bf16[16,2,128]{2,1,0:T(2,128)(2,1)S(1)}, bf16[16,2,128]{2,1,0:T(2,128)(2,1)S(1)}, u32[]{:S(2)}, u32[]{:S(2)}) collective-permute-start(bf16[16,2,128]{2,1,0:T(2,128)(2,1)S(1)} %get-tuple-element.23), channel_id=1, source_target_pairs={{0,1},{1,2},{2,3},{3,4},{4,5},{5,6},{6,7},{7,8},{8,9},{9,10},{10,1... | collective-permute-start | bytes 24584 | tf_op jit(solution)/shard_map/ppermute | solution.py:42
  277.4 8.2 %collective-permute-start.5 = (bf16[2,80,128]{2,1,0:T(8,128)(2,1)S(1)}, bf16[2,80,128]{2,1,0:T(8,128)(2,1)S(1)}, u32[]{:S(2)}, u32[]{:S(2)}) collective-permute-start(bf16[2,80,128]{2,1,0:T(8,128)(2,1)S(1)} %get-tuple-element.26), channel_id=1, source_target_pairs={{16,0},{32,16},{48,32},{64,48},{80,64},{96,80},{112,96},{128,112},... | collective-permute-start | bytes 122888 | tf_op jit(solution)/shard_map/ppermute | solution.py:43
  279.3 8.4 %collective-permute-start.4 = (bf16[2,80,128]{2,1,0:T(8,128)(2,1)S(1)}, bf16[2,80,128]{2,1,0:T(8,128)(2,1)S(1)}, u32[]{:S(2)}, u32[]{:S(2)}) collective-permute-start(bf16[2,80,128]{2,1,0:T(8,128)(2,1)S(1)} %get-tuple-element.25), channel_id=1, source_target_pairs={{0,16},{16,32},{32,48},{48,64},{64,80},{80,96},{96,112},{112,128},... | collective-permute-start | bytes 122888 | tf_op jit(solution)/shard_map/ppermute | solution.py:42
  288.5 9.9 %collective-permute-start.7 = (bf16[16,2,128]{2,1,0:T(2,128)(2,1)S(1)}, bf16[16,2,128]{2,1,0:T(2,128)(2,1)S(1)}, u32[]{:S(2)}, u32[]{:S(2)}) collective-permute-start(bf16[16,2,128]{2,1,0:T(2,128)(2,1)S(1)} %get-tuple-element.20), channel_id=1, source_target_pairs={{1,0},{2,1},{3,2},{4,3},{5,4},{6,5},{7,6},{8,7},{9,8},{10,9},{11,1... | collective-permute-start | bytes 24584 | tf_op jit(solution)/shard_map/ppermute | solution.py:43
  291.1 7.4 %collective-permute-start.6 = (bf16[16,2,128]{2,1,0:T(2,128)(2,1)S(1)}, bf16[16,2,128]{2,1,0:T(2,128)(2,1)S(1)}, u32[]{:S(2)}, u32[]{:S(2)}) collective-permute-start(bf16[16,2,128]{2,1,0:T(2,128)(2,1)S(1)} %get-tuple-element.19), channel_id=1, source_target_pairs={{0,1},{1,2},{2,3},{3,4},{4,5},{5,6},{6,7},{7,8},{8,9},{9,10},{10,1... | collective-permute-start | bytes 24584 | tf_op jit(solution)/shard_map/ppermute | solution.py:42
  291.1 8.2 %collective-permute-start.9 = (bf16[2,80,128]{2,1,0:T(8,128)(2,1)S(1)}, bf16[2,80,128]{2,1,0:T(8,128)(2,1)S(1)}, u32[]{:S(2)}, u32[]{:S(2)}) collective-permute-start(bf16[2,80,128]{2,1,0:T(8,128)(2,1)S(1)} %get-tuple-element.22), channel_id=1, source_target_pairs={{16,0},{32,16},{48,32},{64,48},{80,64},{96,80},{112,96},{128,112},... | collective-permute-start | bytes 122888 | tf_op jit(solution)/shard_map/ppermute | solution.py:43
  294.7 8.3 %collective-permute-start.8 = (bf16[2,80,128]{2,1,0:T(8,128)(2,1)S(1)}, bf16[2,80,128]{2,1,0:T(8,128)(2,1)S(1)}, u32[]{:S(2)}, u32[]{:S(2)}) collective-permute-start(bf16[2,80,128]{2,1,0:T(8,128)(2,1)S(1)} %get-tuple-element.21), channel_id=1, source_target_pairs={{0,16},{16,32},{32,48},{48,64},{64,80},{80,96},{96,112},{112,128},... | collective-permute-start | bytes 122888 | tf_op jit(solution)/shard_map/ppermute | solution.py:42
  303.7 9.5 %collective-permute-start.11 = (bf16[16,2,128]{2,1,0:T(2,128)(2,1)S(1)}, bf16[16,2,128]{2,1,0:T(2,128)(2,1)S(1)}, u32[]{:S(2)}, u32[]{:S(2)}) collective-permute-start(bf16[16,2,128]{2,1,0:T(2,128)(2,1)S(1)} %get-tuple-element.16), channel_id=1, source_target_pairs={{1,0},{2,1},{3,2},{4,3},{5,4},{6,5},{7,6},{8,7},{9,8},{10,9},{11,1... | collective-permute-start | bytes 24584 | tf_op jit(solution)/shard_map/ppermute | solution.py:43
  305.6 7.6 %collective-permute-start.10 = (bf16[16,2,128]{2,1,0:T(2,128)(2,1)S(1)}, bf16[16,2,128]{2,1,0:T(2,128)(2,1)S(1)}, u32[]{:S(2)}, u32[]{:S(2)}) collective-permute-start(bf16[16,2,128]{2,1,0:T(2,128)(2,1)S(1)} %get-tuple-element.15), channel_id=1, source_target_pairs={{0,1},{1,2},{2,3},{3,4},{4,5},{5,6},{6,7},{7,8},{8,9},{9,10},{10,1... | collective-permute-start | bytes 24584 | tf_op jit(solution)/shard_map/ppermute | solution.py:42
  305.6 8.4 %collective-permute-start.13 = (bf16[2,80,128]{2,1,0:T(8,128)(2,1)S(1)}, bf16[2,80,128]{2,1,0:T(8,128)(2,1)S(1)}, u32[]{:S(2)}, u32[]{:S(2)}) collective-permute-start(bf16[2,80,128]{2,1,0:T(8,128)(2,1)S(1)} %get-tuple-element.18), channel_id=1, source_target_pairs={{16,0},{32,16},{48,32},{64,48},{80,64},{96,80},{112,96},{128,112},... | collective-permute-start | bytes 122888 | tf_op jit(solution)/shard_map/ppermute | solution.py:43
  311.3 8.3 %collective-permute-start.12 = (bf16[2,80,128]{2,1,0:T(8,128)(2,1)S(1)}, bf16[2,80,128]{2,1,0:T(8,128)(2,1)S(1)}, u32[]{:S(2)}, u32[]{:S(2)}) collective-permute-start(bf16[2,80,128]{2,1,0:T(8,128)(2,1)S(1)} %get-tuple-element.17), channel_id=1, source_target_pairs={{0,16},{16,32},{32,48},{48,64},{64,80},{80,96},{96,112},{112,128},... | collective-permute-start | bytes 122888 | tf_op jit(solution)/shard_map/ppermute | solution.py:42
  320.3 9.3 %collective-permute-start.15 = (bf16[16,2,128]{2,1,0:T(2,128)(2,1)S(1)}, bf16[16,2,128]{2,1,0:T(2,128)(2,1)S(1)}, u32[]{:S(2)}, u32[]{:S(2)}) collective-permute-start(bf16[16,2,128]{2,1,0:T(2,128)(2,1)S(1)} %get-tuple-element.12), channel_id=1, source_target_pairs={{1,0},{2,1},{3,2},{4,3},{5,4},{6,5},{7,6},{8,7},{9,8},{10,9},{11,1... | collective-permute-start | bytes 24584 | tf_op jit(solution)/shard_map/ppermute | solution.py:43
  322.2 7.4 %collective-permute-start.14 = (bf16[16,2,128]{2,1,0:T(2,128)(2,1)S(1)}, bf16[16,2,128]{2,1,0:T(2,128)(2,1)S(1)}, u32[]{:S(2)}, u32[]{:S(2)}) collective-permute-start(bf16[16,2,128]{2,1,0:T(2,128)(2,1)S(1)} %get-tuple-element.11), channel_id=1, source_target_pairs={{0,1},{1,2},{2,3},{3,4},{4,5},{5,6},{6,7},{7,8},{8,9},{9,10},{10,1... | collective-permute-start | bytes 24584 | tf_op jit(solution)/shard_map/ppermute | solution.py:42
  322.2 8.2 %collective-permute-start.17 = (bf16[2,80,128]{2,1,0:T(8,128)(2,1)S(1)}, bf16[2,80,128]{2,1,0:T(8,128)(2,1)S(1)}, u32[]{:S(2)}, u32[]{:S(2)}) collective-permute-start(bf16[2,80,128]{2,1,0:T(8,128)(2,1)S(1)} %get-tuple-element.14), channel_id=1, source_target_pairs={{16,0},{32,16},{48,32},{64,48},{80,64},{96,80},{112,96},{128,112},... | collective-permute-start | bytes 122888 | tf_op jit(solution)/shard_map/ppermute | solution.py:43
  327.0 8.3 %collective-permute-start.16 = (bf16[2,80,128]{2,1,0:T(8,128)(2,1)S(1)}, bf16[2,80,128]{2,1,0:T(8,128)(2,1)S(1)}, u32[]{:S(2)}, u32[]{:S(2)}) collective-permute-start(bf16[2,80,128]{2,1,0:T(8,128)(2,1)S(1)} %get-tuple-element.13), channel_id=1, source_target_pairs={{0,16},{16,32},{32,48},{48,64},{64,80},{80,96},{96,112},{112,128},... | collective-permute-start | bytes 122888 | tf_op jit(solution)/shard_map/ppermute | solution.py:42
  335.6 1.3 copy-start.1
